TPU v7x, 32 devices: a whole 2x2x4 slice. The times are simulated.
32 devices in a mesh: band: 8 (over y, x, core), gblk: 4 (over z).
Axes of the slice: x: 2, y: 2, z: 4, core: 2. Of those that a mesh axis runs over, the one named last changes fastest.
Arguments:
- eps_inv: bfloat16 [2, 2, 8, 4, 512, 16384], P(None, None, None, 'gblk', None, 'band'), may hold values from -6 to 6
- pair_elements: bfloat16 [2, 1, 16, 16384], P(None, None, 'band'), may hold values from -0.046875 to 0.046875
Outputs:
- sigma_terms: float32 [2, 2, 1, 16], P(None, None, None, 'band')
All inputs are finite; a program needn't handle non-finite values.
Results may differ from a plain program's by a relative error of at most 0.0003.
Values may be sent and summed in bfloat16 or wider, within the bound.
No kernel may reach another device: no remote copies, remote signals or barrier semaphores. Data moves between devices by JAX's collectives and lax.ppermute only.
A program may use at most 128 MiB of HBM per device.

v0:
```python
import jax
import jax.numpy as jnp
from jax import lax
from jax.sharding import PartitionSpec as P


def shards(eps_inv, pair_elements):
    group_count = lax.axis_size("gblk")
    group_index = lax.axis_index("gblk")
    freqs = eps_inv.shape[0]
    rounds = eps_inv.shape[2]
    tile_rows = eps_inv.shape[4]
    width = eps_inv.shape[5]
    states = pair_elements.shape[1]
    local_bands = pair_elements.shape[2]
    columns = lax.all_to_all(pair_elements, "band", split_axis=3, concat_axis=2, tiled=True)
    all_bands = columns.shape[2]
    blocks = eps_inv.reshape(freqs, 2, -1, width)
    shaped = pair_elements.reshape(2, states, local_bands, rounds, group_count, tile_rows)
    picked = lax.dynamic_slice_in_dim(shaped, group_index, 1, 4)
    row_local = picked.reshape(2, states, local_bands, rounds * tile_rows)
    flat = columns.reshape(-1, width)
    contract_last = (((1,), (1,)), ((), ()))
    images = []
    for frequency in range(freqs):
        along_a = lax.dot_general(
            flat, blocks[frequency, 0], contract_last, preferred_element_type=jnp.float32
        )
        along_b = lax.dot_general(
            flat, blocks[frequency, 1], contract_last, preferred_element_type=jnp.float32
        )
        along_a = along_a.reshape(2, states, all_bands, -1)
        along_b = along_b.reshape(2, states, all_bands, -1)
        images.append(jnp.stack([along_a[0] - along_b[1], along_a[1] + along_b[0]]))
    image = jnp.stack(images)
    piece = lax.all_gather(row_local, "band", axis=2, tiled=True)
    real_part = piece[0].astype(jnp.float32)
    imag_part = piece[1].astype(jnp.float32)
    sigma_re = jnp.sum(real_part * image[:, 0] + imag_part * image[:, 1], axis=-1)
    sigma_im = jnp.sum(real_part * image[:, 1] - imag_part * image[:, 0], axis=-1)
    partial_sigma = jnp.stack([sigma_re, sigma_im], axis=1)
    reduced = lax.psum_scatter(partial_sigma, "band", scatter_dimension=3, tiled=True)
    return lax.psum(reduced, "gblk")


def solution(mesh):
    placed = (P(None, None, None, "gblk", None, "band"), P(None, None, "band", None))
    return jax.shard_map(
        shards, mesh=mesh, in_specs=placed, out_specs=P(None, None, None, "band"), check_vma=False
    )
```

profile of v0, /device:TPU:0, one launch (start us, length us, event | category | flops | bytes accessed | tf_op | source)
XLA Modules:
  0.0 138.5 jit_solution(16395664978475546550)
XLA Ops:
  0.0 15.4 %copy.24 = bf16[2,1,2,16384]{2,0,1,3:T(2,128)(2,1)} copy(bf16[2,1,2,16384]{3,2,1,0:T(2,128)(2,1)} %param.3) | data formatting | bytes 262144 | tf_op args[1]
  15.5 13.7 %reshape.124 = bf16[8,2,4096]{2,1,0:T(2,128)(2,1)} reshape(bf16[16384,1,2,2]{3,2,1,0:T(2,128)(2,1)} %bitcast.63) | data formatting | bytes 262144
  29.2 5.2 %all-to-all-start = ((bf16[8,2,4096]{2,1,0:T(2,128)(2,1)}), bf16[8,2,4096]{2,1,0:T(2,128)(2,1)S(1)}, u32[]{:S(2)}, u32[]{:S(2)}) async-start(bf16[8,2,4096]{2,1,0:T(2,128)(2,1)} %reshape.124), calls=%async_computation | async-start | bytes 262144 | tf_op jit(solution)/shard_map/all_to_all | solution.py:16
  34.4 0.1 reshape.113
  34.5 0.2 dynamic-slice_reduce_fusion
  34.8 9.8 %all_gather.3 = bf16[2,1,16,4096]{3,0,1,2:T(2,128)(2,1)S(1)} all-gather(bf16[2,1,2,4096]{3,0,1,2:T(2,128)(2,1)S(1)} %copy.23), channel_id=1, replica_groups=mesh['band'=8,'gblk'=4] {'band'}, dimensions={2}, use_global_device_ids=true | all-gather | bytes 294912 | tf_op jit(solution)/shard_map/all_gather | solution.py:36
  44.6 0.5 slice_convert_fusion.1
  45.1 0.3 copy_bitcast_fusion
  45.4 0.6 dynamic-slice
  46.7 19.1 %reshape.125 = bf16[16384,1,2,2]{3,2,1,0:T(2,128)(2,1)} reshape(bf16[8,2,4096]{2,1,0:T(2,128)(2,1)S(1)} %all-to-all-done) | data formatting | bytes 262144
  65.8 11.9 %copy.29 = bf16[2,1,2,8,2048]{4,3,2,0,1:T(8,128)(2,1)S(1)} copy(bf16[2,1,2,8,2048]{2,0,4,3,1:T(2,128)(2,1)} %bitcast.62) | data formatting | bytes 262144 | tf_op jit(solution)/shard_map/all_to_all | solution.py:16
  77.6 0.1 copy.26
  77.8 0.1 reshape.115
  77.9 8.6 %fusion.2 = f32[32,4096]{1,0:T(8,128)S(1)} fusion(bf16[32,2048]{1,0:T(8,128)(2,1)S(1)} %reshape.115, bf16[2,2,4096,2048]{3,2,1,0:T(8,128)(2,1)} %bitcast.2), kind=kOutput, calls=%fused_computation.5 | convolution fusion | flops 536870912 | bytes 17432576 | tf_op jit(solution)/shard_map/dot_general | solution.py:29
  86.4 8.6 %fusion.3 = f32[32,4096]{1,0:T(8,128)S(1)} fusion(bf16[32,2048]{1,0:T(8,128)(2,1)S(1)} %reshape.115, bf16[2,2,4096,2048]{3,2,1,0:T(8,128)(2,1)} %bitcast.2), kind=kOutput, calls=%fused_computation.7 | convolution fusion | flops 536870912 | bytes 17432576 | tf_op jit(solution)/shard_map/dot_general | solution.py:26
  95.0 8.6 %fusion = f32[32,4096]{1,0:T(8,128)S(1)} fusion(bf16[32,2048]{1,0:T(8,128)(2,1)S(1)} %reshape.115, bf16[2,2,4096,2048]{3,2,1,0:T(8,128)(2,1)} %bitcast.2), kind=kOutput, calls=%fused_computation.1 | convolution fusion | flops 536870912 | bytes 17432576 | tf_op jit(solution)/shard_map/dot_general | solution.py:29
  103.6 8.6 %fusion.1 = f32[32,4096]{1,0:T(8,128)S(1)} fusion(bf16[32,2048]{1,0:T(8,128)(2,1)S(1)} %reshape.115, bf16[2,2,4096,2048]{3,2,1,0:T(8,128)(2,1)} %bitcast.2), kind=kOutput, calls=%fused_computation.3 | convolution fusion | flops 536870912 | bytes 17432576 | tf_op jit(solution)/shard_map/dot_general | solution.py:26
  112.2 0.1 fusion.10
  112.3 0.1 fusion.8
  112.4 0.2 add_reduce_fusion
  112.7 13.2 %all-reduce = f32[2,2,1,16]{3,0,2,1:T(2,128)S(1)} all-reduce(f32[2,2,1,16]{3,0,2,1:T(2,128)S(1)} %pad_maximum_fusion.1), channel_id=2, replica_groups=mesh['band'=8,'gblk'=4] {'band'}, use_global_device_ids=true, to_apply=%region_2.0.clone | all-reduce | flops 64 | bytes 512
  125.9 0.1 constant_dynamic-slice_fusion
  125.9 11.9 %psum.7 = f32[2,2,1,2]{3,0,2,1:T(2,128)S(1)} all-reduce(f32[2,2,1,2]{3,0,2,1:T(2,128)S(1)} %constant_dynamic-slice_fusion), channel_id=1, replica_groups=mesh['band'=8,'gblk'=4] {'gblk'}, use_global_device_ids=true, to_apply=%region_3.0 | all-reduce | flops 8 | bytes 64 | tf_op jit(solution)/shard_map/psum | solution.py:43
  137.9 0.6 copy.28
  (10 shorter events, 0.1 us)
Async XLA Ops:
  0.0 45.4 %copy-start.1 = (u32[32]{0:T(128)S(1)}, u32[32]{0:T(128)}, u32[]{:S(2)}) copy-start(u32[32]{0:T(128)} %constant.14) | copy-start | bytes 388
  0.0 34.4 %copy-start = (bf16[2,1,2,16384]{3,2,1,0:T(2,128)(2,1)S(1)}, bf16[2,1,2,16384]{3,2,1,0:T(2,128)(2,1)}, u32[]{:S(2)}) copy-start(bf16[2,1,2,16384]{3,2,1,0:T(2,128)(2,1)} %param.3) | copy-start | bytes 393220
  29.2 17.5 %all-to-all-start = ((bf16[8,2,4096]{2,1,0:T(2,128)(2,1)}), bf16[8,2,4096]{2,1,0:T(2,128)(2,1)S(1)}, u32[]{:S(2)}, u32[]{:S(2)}) async-start(bf16[8,2,4096]{2,1,0:T(2,128)(2,1)} %reshape.124), calls=%async_computation | async-start | bytes 262144 | tf_op jit(solution)/shard_map/all_to_all | solution.py:16
where the time goes:
time: 140 us; the launch traced here: 138 us
  local copies, waits for them, and re-layouts  62.2 us (44%)
  blocking collectives  35 us (25%)
  matrix products  34.3 us (24%)
  starting transfers between devices  5.2 us (4%)
    unnamed x10, local copies, waits for them, and re-layouts  49.2 us
    dot_general x2, matrix products, shards(): lax.dot_general(flat, blocks[frequency, 0], contract_last, preferred_elem...  17.2 us
    dot_general x2, matrix products, shards(): lax.dot_general(flat, blocks[frequency, 1], contract_last, preferred_elem...  17.1 us
    unnamed x1, blocking collectives  13.2 us
    all_to_all x2, local copies, waits for them, and re-layouts, shards(): lax.all_to_all(pair_elements, 'band', split_axis=3, concat_axis=2, tiled=...  12 us
    psum x1, blocking collectives, shards(): return lax.psum(reduced, 'gblk')  11.9 us
    all_gather x1, blocking collectives, shards(): piece = lax.all_gather(row_local, 'band', axis=2, tiled=True)  9.81 us
    all_to_all x1, starting transfers between devices, shards(): lax.all_to_all(pair_elements, 'band', split_axis=3, concat_axis=2, tiled=...  5.2 us
  transfers between devices with their start and end apart: 1, of which 0 were waited for; matrix products, arithmetic and copies ran while one was open for 1% of the time, Pallas kernels for 0%

commit v1 on v0

--- a/solution.py
+++ b/solution.py
@@ -13,7 +13,12 @@
     width = eps_inv.shape[5]
     states = pair_elements.shape[1]
     local_bands = pair_elements.shape[2]
-    columns = lax.all_to_all(pair_elements, "band", split_axis=3, concat_axis=2, tiled=True)
+    columns = jnp.concatenate(
+        lax.all_to_all(
+            jnp.stack(jnp.split(pair_elements, lax.axis_size("band"), axis=3)), "band", 0, 0
+        ),
+        axis=2,
+    )
     all_bands = columns.shape[2]
     blocks = eps_inv.reshape(freqs, 2, -1, width)
     shaped = pair_elements.reshape(2, states, local_bands, rounds, group_count, tile_rows)

time: 140 us -> 91.2 us (0.65)
  local copies, waits for them, and re-layouts: 62.2 us -> 14.2 us
    unnamed x10, local copies, waits for them, and re-layouts: 49.2 us -> 10.9 us
    all_to_all x2 -> x0, local copies, waits for them, and re-layouts: 12 us -> none  [shards(): lax.all_to_all(pair_elements, 'band', split_axis=3, concat_axis=2, tiled=...]
  transfers between devices with their start and end apart: 1 -> 1, of which waited for: 0 -> 0; matrix products, arithmetic and copies ran while one was open for 1% -> 4% of each run, Pallas kernels for 0% -> 0%
where the time goes in v1:
time: 91.2 us; the launch traced here: 90.4 us
  blocking collectives  35 us (38%)
  matrix products  34.3 us (38%)
  local copies, waits for them, and re-layouts  14.2 us (16%)
  starting transfers between devices  5.2 us (6%)
  other arithmetic  1.01 us (1%)
    dot_general x2, matrix products, shards(): lax.dot_general(flat, blocks[frequency, 0], contract_last, preferred_elem...  17.2 us
    dot_general x2, matrix products, shards(): lax.dot_general(flat, blocks[frequency, 1], contract_last, preferred_elem...  17.1 us
    unnamed x1, blocking collectives  13.2 us
    psum x1, blocking collectives, shards(): return lax.psum(reduced, 'gblk')  11.9 us
    unnamed x10, local copies, waits for them, and re-layouts  10.9 us
    all_gather x1, blocking collectives, shards(): piece = lax.all_gather(row_local, 'band', axis=2, tiled=True)  9.81 us
    all_to_all x1, starting transfers between devices, shards(): lax.all_to_all(jnp.stack(jnp.split(pair_elements, lax.axis_size('band'),...  5.2 us
  transfers between devices with their start and end apart: 1, of which 0 were waited for; matrix products, arithmetic and copies ran while one was open for 4% of the time, Pallas kernels for 0%

profile of v1, /device:TPU:0, one launch (start us, length us, event | category | flops | bytes accessed | tf_op | source)
XLA Modules:
  0.0 90.4 jit_solution(16909850481913745224)
XLA Ops:
  0.0 1.3 %constant_dynamic-update-slice_fusion.7 = bf16[8,2,1,2,2048]{4,3,1,2,0:T(2,128)(2,1)} fusion(bf16[2,1,2,16384]{3,2,0,1:T(2,128)(2,1)} %bitcast.96), kind=kLoop, calls=%fused_computation.38 | loop fusion | bytes 32768
  1.3 1.3 %constant_dynamic-update-slice_fusion.6 = bf16[8,2,1,2,2048]{4,3,1,2,0:T(2,128)(2,1)} fusion(bf16[8,2,1,2,2048]{4,3,1,2,0:T(2,128)(2,1)} %constant_dynamic-update-slice_fusion.7, bf16[2,1,2,16384]{3,2,0,1:T(2,128)(2,1)} %bitcast.97), kind=kLoop, calls=%fused_computation.37 | loop fusion | bytes 32768
  2.7 1.3 %constant_dynamic-update-slice_fusion.5 = bf16[8,2,1,2,2048]{4,3,1,2,0:T(2,128)(2,1)} fusion(bf16[8,2,1,2,2048]{4,3,1,2,0:T(2,128)(2,1)} %constant_dynamic-update-slice_fusion.6, bf16[2,1,2,16384]{3,2,0,1:T(2,128)(2,1)} %bitcast.98), kind=kLoop, calls=%fused_computation.36 | loop fusion | bytes 32768
  4.0 1.3 %constant_dynamic-update-slice_fusion.4 = bf16[8,2,1,2,2048]{4,3,1,2,0:T(2,128)(2,1)} fusion(bf16[8,2,1,2,2048]{4,3,1,2,0:T(2,128)(2,1)} %constant_dynamic-update-slice_fusion.5, bf16[2,1,2,16384]{3,2,0,1:T(2,128)(2,1)} %bitcast.99), kind=kLoop, calls=%fused_computation.35 | loop fusion | bytes 32768
  5.3 1.3 %constant_dynamic-update-slice_fusion.3 = bf16[8,2,1,2,2048]{4,3,1,2,0:T(2,128)(2,1)} fusion(bf16[8,2,1,2,2048]{4,3,1,2,0:T(2,128)(2,1)} %constant_dynamic-update-slice_fusion.4, bf16[2,1,2,16384]{3,2,0,1:T(2,128)(2,1)} %bitcast.100), kind=kLoop, calls=%fused_computation.34 | loop fusion | bytes 32768
  6.6 1.3 %constant_dynamic-update-slice_fusion.2 = bf16[8,2,1,2,2048]{4,3,1,2,0:T(2,128)(2,1)} fusion(bf16[8,2,1,2,2048]{4,3,1,2,0:T(2,128)(2,1)} %constant_dynamic-update-slice_fusion.3, bf16[2,1,2,16384]{3,2,1,0:T(2,128)(2,1)} %param.3), kind=kLoop, calls=%fused_computation.33 | loop fusion | bytes 32768
  8.0 1.3 %constant_dynamic-update-slice_fusion.1 = bf16[8,2,1,2,2048]{4,3,1,2,0:T(2,128)(2,1)} fusion(bf16[8,2,1,2,2048]{4,3,1,2,0:T(2,128)(2,1)} %constant_dynamic-update-slice_fusion.2, bf16[2,1,2,16384]{3,2,0,1:T(2,128)(2,1)} %bitcast.101), kind=kLoop, calls=%fused_computation.32 | loop fusion | bytes 32768
  9.3 1.3 %constant_dynamic-update-slice_fusion = bf16[8,2,1,2,2048]{4,3,1,2,0:T(2,128)(2,1)} fusion(bf16[8,2,1,2,2048]{4,3,1,2,0:T(2,128)(2,1)} %constant_dynamic-update-slice_fusion.1, bf16[2,1,2,16384]{3,2,0,1:T(2,128)(2,1)} %bitcast.102), kind=kLoop, calls=%fused_computation.31 | loop fusion | bytes 32768 | tf_op jit(solution)/shard_map/stack | solution.py:18
  10.6 5.2 %all-to-all-start = ((bf16[8,2,1,2,2048]{4,3,1,2,0:T(2,128)(2,1)}), bf16[8,2,1,2,2048]{4,3,1,2,0:T(2,128)(2,1)S(1)}, u32[]{:S(2)}, u32[]{:S(2)}) async-start(bf16[8,2,1,2,2048]{4,3,1,2,0:T(2,128)(2,1)} %constant_dynamic-update-slice_fusion), calls=%async_computation | async-start | bytes 262144 | tf_op jit(solution)/shard_map/all_to_all | solution.py:17
  15.8 1.0 %reshape.112 = bf16[2,1,2,8,4,512]{5,4,3,2,0,1:T(4,128)(2,1)S(1)} reshape(bf16[2,1,2,16384]{3,2,1,0:T(2,128)(2,1)} %param.3) | data formatting | bytes 262144 | tf_op jit(solution)/shard_map/reshape | solution.py:24
  16.8 0.2 dynamic-slice_reduce_fusion
  17.1 9.8 %all_gather.3 = bf16[2,1,16,4096]{3,0,1,2:T(2,128)(2,1)S(1)} all-gather(bf16[2,1,2,4096]{3,0,1,2:T(2,128)(2,1)S(1)} %copy.24), channel_id=1, replica_groups=mesh['band'=8,'gblk'=4] {'band'}, dimensions={2}, use_global_device_ids=true | all-gather | bytes 294912 | tf_op jit(solution)/shard_map/all_gather | solution.py:41
  26.9 0.5 slice_convert_fusion.1
  27.5 0.3 copy_bitcast_fusion
  27.8 1.2 %dynamic-slice = u32[1]{0:T(128)} dynamic-slice(u32[32]{0:T(128)} %constant.14, u32[]{:T(128)S(6)} %add.31), dynamic_slice_sizes={1} | dynamic-slice | bytes 12
  29.8 8.6 %fusion.2 = f32[32,4096]{1,0:T(8,128)S(1)} fusion(bf16[32,2048]{1,0:T(8,128)(2,1)S(1)} %reshape_reshape.3, bf16[2,2,4096,2048]{3,2,1,0:T(8,128)(2,1)} %bitcast.16), kind=kOutput, calls=%fused_computation.5 | convolution fusion | flops 536870912 | bytes 17432576 | tf_op jit(solution)/shard_map/dot_general | solution.py:34
  38.4 8.6 %fusion.3 = f32[32,4096]{1,0:T(8,128)S(1)} fusion(bf16[32,2048]{1,0:T(8,128)(2,1)S(1)} %reshape_reshape.3, bf16[2,2,4096,2048]{3,2,1,0:T(8,128)(2,1)} %bitcast.16), kind=kOutput, calls=%fused_computation.7 | convolution fusion | flops 536870912 | bytes 17432576 | tf_op jit(solution)/shard_map/dot_general | solution.py:31
  47.0 8.6 %fusion = f32[32,4096]{1,0:T(8,128)S(1)} fusion(bf16[32,2048]{1,0:T(8,128)(2,1)S(1)} %reshape_reshape.3, bf16[2,2,4096,2048]{3,2,1,0:T(8,128)(2,1)} %bitcast.16), kind=kOutput, calls=%fused_computation.1 | convolution fusion | flops 536870912 | bytes 17432576 | tf_op jit(solution)/shard_map/dot_general | solution.py:34
  55.6 8.6 %fusion.1 = f32[32,4096]{1,0:T(8,128)S(1)} fusion(bf16[32,2048]{1,0:T(8,128)(2,1)S(1)} %reshape_reshape.3, bf16[2,2,4096,2048]{3,2,1,0:T(8,128)(2,1)} %bitcast.16), kind=kOutput, calls=%fused_computation.3 | convolution fusion | flops 536870912 | bytes 17432576 | tf_op jit(solution)/shard_map/dot_general | solution.py:31
  64.1 0.1 fusion.10
  64.4 0.2 add_reduce_fusion
  64.6 13.2 %all-reduce = f32[2,2,1,16]{3,0,2,1:T(2,128)S(1)} all-reduce(f32[2,2,1,16]{3,0,2,1:T(2,128)S(1)} %pad_maximum_fusion.1), channel_id=2, replica_groups=mesh['band'=8,'gblk'=4] {'band'}, use_global_device_ids=true, to_apply=%region_2.0.clone | all-reduce | flops 64 | bytes 512
  77.9 11.9 %psum.7 = f32[2,2,1,2]{3,0,2,1:T(2,128)S(1)} all-reduce(f32[2,2,1,2]{3,0,2,1:T(2,128)S(1)} %constant_dynamic-slice_fusion), channel_id=1, replica_groups=mesh['band'=8,'gblk'=4] {'gblk'}, use_global_device_ids=true, to_apply=%region_3.0 | all-reduce | flops 8 | bytes 64 | tf_op jit(solution)/shard_map/psum | solution.py:48
  89.9 0.6 copy.34
  (10 shorter events, 0.4 us)
Async XLA Ops:
  10.6 19.1 %all-to-all-start = ((bf16[8,2,1,2,2048]{4,3,1,2,0:T(2,128)(2,1)}), bf16[8,2,1,2,2048]{4,3,1,2,0:T(2,128)(2,1)S(1)}, u32[]{:S(2)}, u32[]{:S(2)}) async-start(bf16[8,2,1,2,2048]{4,3,1,2,0:T(2,128)(2,1)} %constant_dynamic-update-slice_fusion), calls=%async_computation | async-start | bytes 262144 | tf_op jit(solution)/shard_map/all_to_all | solution.py:17
